TPU v7x, 32 devices: a whole 2x2x4 slice. The times are simulated.
32 devices in a mesh: parts: 2 (over x), snp: 16 (over z, y, core).
Axes of the slice: x: 2, y: 2, z: 4, core: 2. Of those that a mesh axis runs over, the one named last changes fastest.
Arguments:
- local_block: float32 [32768, 1024], P(('parts', 'snp')), parts along dimension 0, may hold values from -1 to 1, as said below
- next_block: float32 [32768, 1024], P(('parts', 'snp')), parts along dimension 0, may hold values from -1 to 1, as said below
- shrinkage: float32 [64, 1], replicated, may hold values from 0.3 to 1
- marginal: float32 [64, 32768], P(None, ('parts', 'snp')), parts along dimension 1, may hold values from -12 to 12
- warm_start: float32 [64, 32768], P(None, ('parts', 'snp')), parts along dimension 1, may hold values from -3 to 3
Outputs:
- solution: float32 [64, 32768], P(None, ('parts', 'snp')), parts along dimension 1
- residual: float32 [64, 32768], P(None, ('parts', 'snp')), parts along dimension 1
There are 2 independent parts, one for each index of `parts`. A program takes and returns all parts, laid end to end along the dimension named above; an argument that names none is the same for every part. Nothing has to cross between parts.
Inputs may be any that keep to these rules, and one draw needn't show every extreme that they name: `local_block`: each 1024 x 1024 block of rows is symmetric with ones on its diagonal. `next_block`: inside each 1024 x 1024 block of rows, entries whose column index exceeds the row index are zero; the last block of rows is zero.
All inputs are finite; a program needn't handle non-finite values.
Results may differ from a plain program's by a relative error of at most 0.0003.
Values sent between devices are 32-bit elements; how exact they have to be, the bound alone decides.
A program may use at most 64 MiB of HBM per device.

v0:
```python
import jax
import jax.numpy as jnp
from jax import lax
from jax.sharding import PartitionSpec as P

ITERS = 3


HIGH = lax.Precision.HIGHEST


def shifted(block, axis, distance):
    devices = range(lax.axis_size(axis))
    route = [(i - distance, i) for i in devices if i - distance in devices]
    return lax.ppermute(block, axis, route)


def product(left, right):
    return jnp.dot(left, right, precision=HIGH, preferred_element_type=jnp.float32)


def product_across(left, right):
    return lax.dot_general(
        left, right, (((1,), (1,)), ((), ())), precision=HIGH, preferred_element_type=jnp.float32
    )


def paired(residual, image):
    return lax.psum(
        (
            jnp.sum(residual * residual, axis=1, keepdims=True),
            jnp.sum(residual * image, axis=1, keepdims=True),
        ),
        "snp",
    )


def on_device(local_block, next_block, shrinkage, marginal, warm_start):

    def operate(field):
        upper = shifted(field, "snp", -1)
        lower = shifted(product(field, next_block), "snp", 1)
        total = product(field, local_block) + product_across(upper, next_block) + lower
        return total + shrinkage * field

    solution = warm_start
    residual = marginal - operate(warm_start)
    image = operate(residual)
    norm_now, curve = paired(residual, image)
    alpha = norm_now / curve
    direction, along = (residual, image)
    for step in range(ITERS):
        solution = solution + alpha * direction
        residual = residual - alpha * along
        if step + 1 < ITERS:
            image = operate(residual)
            norm_next, curve = paired(residual, image)
            ratio = norm_next / norm_now
            alpha = norm_next / (curve - ratio * norm_next / alpha)
            direction = residual + ratio * direction
            along = image + ratio * along
            norm_now = norm_next
    return (solution, residual)


def solution(mesh):
    return jax.shard_map(
        on_device,
        mesh=mesh,
        in_specs=(
            P(("parts", "snp"), None),
            P(("parts", "snp"), None),
            P(),
            P(None, ("parts", "snp")),
            P(None, ("parts", "snp")),
        ),
        out_specs=(P(None, ("parts", "snp")), P(None, ("parts", "snp"))),
        check_vma=False,
    )
```

profile of v0, /device:TPU:0, one launch (start us, length us, event | category | flops | bytes accessed | tf_op | source)
XLA Modules:
  0.0 163.6 jit_solution(8602006641580616598)
XLA Ops:
  0.6 0.0 copy-start.6
  0.6 0.0 copy-start
  0.7 0.0 copy-start.8
  0.7 0.0 copy-start.7
  0.7 1.6 collective-permute-start
  2.2 4.9 %fusion.11 = f32[64,1024]{1,0:T(8,128)S(1)} fusion(f32[64,1024]{1,0:T(8,128)} %param.9, f32[1024,1024]{1,0:T(8,128)} %param.6), kind=kOutput, calls=%fused_computation.30 | convolution fusion | flops 805306368 | bytes 4718592 | tf_op jit(solution)/shard_map/dot_general | solution.py:19
  7.2 3.0 %collective-permute-start.1 = (f32[64,1024]{1,0:T(8,128)S(1)}, f32[64,1024]{1,0:T(8,128)S(1)}, u32[]{:S(2)}, u32[]{:S(2)}) collective-permute-start(f32[64,1024]{1,0:T(8,128)S(1)} %fusion.11), channel_id=1, source_target_pairs={{0,1},{1,2},{2,3},{3,4},{4,5},{5,6},{6,7},{7,8},{8,9},{9,10},{10,1... | collective-permute-start | bytes 786440 | tf_op jit(solution)/shard_map/ppermute | solution.py:15
  10.2 0.0 copy-done.6
  10.2 4.8 %fusion.10 = f32[64,1024]{1,0:T(8,128)S(1)} fusion(f32[64,1024]{1,0:T(8,128)S(1)} %copy-done.6, f32[1024,1024]{1,0:T(8,128)} %param.5), kind=kOutput, calls=%fused_computation.29 | convolution fusion | flops 805306368 | bytes 4718592 | tf_op jit(solution)/shard_map/dot_general | solution.py:19
  15.1 0.0 collective-permute-done.1
  15.1 0.0 collective-permute-done
  15.1 0.0 copy-done
  15.1 0.0 copy-done.8
  15.1 0.0 copy-done.7
  15.1 4.2 %fusion.8 = f32[64,1024]{1,0:T(8,128)S(1)} fusion(f32[64,1024]{1,0:T(8,128)S(1)} %copy-done.7, f32[64,1024]{1,0:T(8,128)S(1)} %collective-permute-done.1, f32[64,1024]{1,0:T(8,128)S(1)} %fusion.10, f32[64,1024]{1,0:T(8,128)S(1)} %collective-permute-done, f32[1024,1024]{1,0:T(8,128)S(1)} %copy-done, f32[64,1024]{1,0:T(8,128)S(1)} %copy-done.6, ...), kind=kOutput, calls=%fused_computation.12 | convolution fusion | flops 805634048 | bytes 5767424 | tf_op jit(solution)/shard_map/dot_general | solution.py:23
  19.3 0.0 copy-start.3
  19.3 1.6 collective-permute-start.2
  20.9 2.7 %fusion.13 = f32[64,1024]{1,0:T(8,128)S(1)} fusion(f32[64,1024]{1,0:T(8,128)S(1)} %fusion.8, f32[1024,1024]{1,0:T(8,128)S(1)} %copy-done), kind=kOutput, calls=%fused_computation.32 | convolution fusion | flops 805306368 | bytes 4718592 | tf_op jit(solution)/shard_map/dot_general | solution.py:19
  23.5 5.3 %collective-permute-start.3 = (f32[64,1024]{1,0:T(8,128)S(1)}, f32[64,1024]{1,0:T(8,128)S(1)}, u32[]{:S(2)}, u32[]{:S(2)}) collective-permute-start(f32[64,1024]{1,0:T(8,128)S(1)} %fusion.13), channel_id=1, source_target_pairs={{0,1},{1,2},{2,3},{3,4},{4,5},{5,6},{6,7},{7,8},{8,9},{9,10},{10,1... | collective-permute-start | bytes 786440 | tf_op jit(solution)/shard_map/ppermute | solution.py:15
  28.9 0.0 collective-permute-done.2
  28.9 4.2 %fusion.12 = f32[64,1024]{1,0:T(8,128)S(1)} fusion(f32[64,1024]{1,0:T(8,128)S(1)} %collective-permute-done.2, f32[1024,1024]{1,0:T(8,128)S(1)} %copy-done), kind=kOutput, calls=%fused_computation.31 | convolution fusion | flops 805306368 | bytes 4718592 | tf_op jit(solution)/shard_map/dot_general | solution.py:23
  33.0 0.0 collective-permute-done.3
  33.0 0.0 copy-done.3
  33.0 2.8 %multiply_reduce_fusion.4 = (f32[64]{0:T(128)S(1)}, f32[64]{0:T(128)S(1)}, f32[64,1024]{1,0:T(8,128)S(1)}) fusion(f32[64,1024]{1,0:T(8,128)S(1)} %fusion.8, f32[64]{0:T(128)S(1)} %bitcast.40, f32[64,1024]{1,0:T(8,128)S(1)} %collective-permute-done.3, f32[64,1024]{1,0:T(8,128)S(1)} %fusion.12, f32[1024,1024]{1,0:T(8,128)S(1)} %copy-done.3), kind=kOutput, calls=%fused_computation.22 | convolution fusion | flops 805830528 | bytes 5243648 | tf_op jit(solution)/shard_map/dot_general | solution.py:19
  35.8 32.8 %all-reduce.2 = (f32[64,1]{0,1:T(1,128)S(1)}, f32[64,1]{0,1:T(1,128)S(1)}) all-reduce(f32[64,1]{0,1:T(1,128)S(1)} %bitcast.49, f32[64,1]{0,1:T(1,128)S(1)} %bitcast.48), channel_id=1, replica_groups=mesh['parts'=2,'snp'=16] {'snp'}, use_global_device_ids=true, to_apply=%region_1.0 | all-reduce | flops 128 | bytes 1024 | tf_op jit(solution)/shard_map/psum | solution.py:29
  68.6 0.0 copy-start.1
  68.6 0.1 multiply_subtract_fusion.2
  68.7 0.0 copy-start.4
  68.7 1.6 collective-permute-start.4
  70.3 5.6 %fusion.15 = f32[64,1024]{1,0:T(8,128)S(1)} fusion(f32[64,1024]{1,0:T(8,128)S(1)} %multiply_subtract_fusion.2, f32[1024,1024]{1,0:T(8,128)} %param.6), kind=kOutput, calls=%fused_computation.34 | convolution fusion | flops 805306368 | bytes 4718592 | tf_op jit(solution)/shard_map/dot_general | solution.py:19
  75.9 2.5 %collective-permute-start.5 = (f32[64,1024]{1,0:T(8,128)S(1)}, f32[64,1024]{1,0:T(8,128)S(1)}, u32[]{:S(2)}, u32[]{:S(2)}) collective-permute-start(f32[64,1024]{1,0:T(8,128)S(1)} %fusion.15), channel_id=1, source_target_pairs={{0,1},{1,2},{2,3},{3,4},{4,5},{5,6},{6,7},{7,8},{8,9},{9,10},{10,1... | collective-permute-start | bytes 786440 | tf_op jit(solution)/shard_map/ppermute | solution.py:15
  78.4 0.0 collective-permute-done.4
  78.4 0.0 copy-done.1
  78.4 4.2 %fusion.14 = f32[64,1024]{1,0:T(8,128)S(1)} fusion(f32[64,1024]{1,0:T(8,128)S(1)} %collective-permute-done.4, f32[1024,1024]{1,0:T(8,128)S(1)} %copy-done.1), kind=kOutput, calls=%fused_computation.33 | convolution fusion | flops 805306368 | bytes 4718592 | tf_op jit(solution)/shard_map/dot_general | solution.py:23
  82.6 0.0 collective-permute-done.5
  82.6 0.0 copy-done.4
  82.6 2.8 %multiply_reduce_fusion.2 = (f32[64]{0:T(128)S(1)}, f32[64]{0:T(128)S(1)}, f32[64,1024]{1,0:T(8,128)S(1)}) fusion(f32[64,1024]{1,0:T(8,128)S(1)} %multiply_subtract_fusion.2, f32[64]{0:T(128)S(1)} %bitcast.41, f32[64,1024]{1,0:T(8,128)S(1)} %collective-permute-done.5, f32[64,1024]{1,0:T(8,128)S(1)} %fusion.14, f32[1024,1024]{1,0:T(8,128)S(1)} %copy-done.4), kind=kOutput, calls=%fused_computation.19 | convolution fusion | flops 805830528 | bytes 5243648 | tf_op jit(solution)/shard_map/dot_general | solution.py:19
  85.4 29.5 %all-reduce.1 = (f32[64,1]{0,1:T(1,128)S(1)}, f32[64,1]{0,1:T(1,128)S(1)}) all-reduce(f32[64,1]{0,1:T(1,128)S(1)} %bitcast.51, f32[64,1]{0,1:T(1,128)S(1)} %bitcast.50), channel_id=1, replica_groups=mesh['parts'=2,'snp'=16] {'snp'}, use_global_device_ids=true, to_apply=%region_5.0 | all-reduce | flops 128 | bytes 1024 | tf_op jit(solution)/shard_map/psum | solution.py:29
  114.9 0.0 copy-start.5
  114.9 0.1 multiply_subtract_fusion.1
  115.0 0.0 copy-start.2
  115.0 5.0 %fusion.17 = f32[64,1024]{1,0:T(8,128)S(1)} fusion(f32[64,1024]{1,0:T(8,128)S(1)} %multiply_subtract_fusion.1, f32[1024,1024]{1,0:T(8,128)} %param.6), kind=kOutput, calls=%fused_computation.36 | convolution fusion | flops 805306368 | bytes 4718592 | tf_op jit(solution)/shard_map/dot_general | solution.py:19
  120.0 1.3 collective-permute-start.6
  121.3 3.3 %collective-permute-start.7 = (f32[64,1024]{1,0:T(8,128)S(1)}, f32[64,1024]{1,0:T(8,128)S(1)}, u32[]{:S(2)}, u32[]{:S(2)}) collective-permute-start(f32[64,1024]{1,0:T(8,128)S(1)} %fusion.17), channel_id=1, source_target_pairs={{0,1},{1,2},{2,3},{3,4},{4,5},{5,6},{6,7},{7,8},{8,9},{9,10},{10,1... | collective-permute-start | bytes 786440 | tf_op jit(solution)/shard_map/ppermute | solution.py:15
  124.6 0.0 copy-done.5
  124.6 2.6 %fusion.16 = f32[64,1024]{1,0:T(8,128)S(1)} fusion(f32[64,1024]{1,0:T(8,128)S(1)} %multiply_subtract_fusion.1, f32[1024,1024]{1,0:T(8,128)S(1)} %copy-done.5), kind=kOutput, calls=%fused_computation.35 | convolution fusion | flops 805306368 | bytes 4718592 | tf_op jit(solution)/shard_map/dot_general | solution.py:19
  127.3 0.0 collective-permute-done.7
  127.3 0.0 collective-permute-done.6
  127.3 0.0 copy-done.2
  127.3 4.3 %multiply_reduce_fusion = (f32[64]{0:T(128)S(1)}, f32[64]{0:T(128)S(1)}, f32[64,1024]{1,0:T(8,128)S(1)}) fusion(f32[64,1024]{1,0:T(8,128)S(1)} %multiply_subtract_fusion.1, f32[64]{0:T(128)S(1)} %bitcast.42, f32[64,1024]{1,0:T(8,128)S(1)} %collective-permute-done.7, f32[64,1024]{1,0:T(8,128)S(1)} %fusion.16, f32[64,1024]{1,0:T(8,128)S(1)} %collective-permute-done.6, ...), kind=kOutput, calls=%fused_computation.15 | convolution fusion | flops 805830528 | bytes 5505792 | tf_op jit(solution)/shard_map/dot_general | solution.py:23
  131.6 30.9 %all-reduce = (f32[64,1]{0,1:T(1,128)S(1)}, f32[64,1]{0,1:T(1,128)S(1)}) all-reduce(f32[64,1]{0,1:T(1,128)S(1)} %bitcast.47, f32[64,1]{0,1:T(1,128)S(1)} %bitcast.46), channel_id=1, replica_groups=mesh['parts'=2,'snp'=16] {'snp'}, use_global_device_ids=true, to_apply=%region_9.0 | all-reduce | flops 128 | bytes 1024 | tf_op jit(solution)/shard_map/psum | solution.py:29
  162.5 1.0 multiply_subtract_fusion
  (3 shorter events, 0.0 us)
Async XLA Ops:
  0.6 9.6 %copy-start.6 = (f32[64,1024]{1,0:T(8,128)S(1)}, f32[64,1024]{1,0:T(8,128)}, u32[]{:S(2)}) copy-start(f32[64,1024]{1,0:T(8,128)} %param.9) | copy-start | bytes 786436
  0.6 14.4 %copy-start = (f32[1024,1024]{1,0:T(8,128)S(1)}, f32[1024,1024]{1,0:T(8,128)}, u32[]{:S(2)}) copy-start(f32[1024,1024]{1,0:T(8,128)} %param.6) | copy-start | bytes 12582916
  0.7 14.4 %copy-start.8 = (f32[64,1]{0,1:T(1,128)S(1)}, f32[64,1]{0,1:T(1,128)}, u32[]{:S(2)}) copy-start(f32[64,1]{0,1:T(1,128)} %param.7) | copy-start | bytes 772
  0.7 14.4 %copy-start.7 = (f32[64,1024]{1,0:T(8,128)S(1)}, f32[64,1024]{1,0:T(8,128)}, u32[]{:S(2)}) copy-start(f32[64,1024]{1,0:T(8,128)} %param.8) | copy-start | bytes 786436
  0.7 14.4 %collective-permute-start = (f32[64,1024]{1,0:T(8,128)}, f32[64,1024]{1,0:T(8,128)S(1)}, u32[]{:S(2)}, u32[]{:S(2)}) collective-permute-start(f32[64,1024]{1,0:T(8,128)} %param.9), channel_id=1, source_target_pairs={{1,0},{2,1},{3,2},{4,3},{5,4},{6,5},{7,6},{8,7},{9,8},{10,9},{11,1... | collective-permute-start | bytes 786440 | tf_op jit(solution)/shard_map/ppermute | solution.py:15
  7.2 7.9 %collective-permute-start.1 = (f32[64,1024]{1,0:T(8,128)S(1)}, f32[64,1024]{1,0:T(8,128)S(1)}, u32[]{:S(2)}, u32[]{:S(2)}) collective-permute-start(f32[64,1024]{1,0:T(8,128)S(1)} %fusion.11), channel_id=1, source_target_pairs={{0,1},{1,2},{2,3},{3,4},{4,5},{5,6},{6,7},{7,8},{8,9},{9,10},{10,1... | collective-permute-start | bytes 786440 | tf_op jit(solution)/shard_map/ppermute | solution.py:15
  19.3 13.7 %copy-start.3 = (f32[1024,1024]{1,0:T(8,128)S(1)}, f32[1024,1024]{1,0:T(8,128)}, u32[]{:S(2)}) copy-start(f32[1024,1024]{1,0:T(8,128)} %param.5) | copy-start | bytes 12582916
  19.3 9.6 %collective-permute-start.2 = (f32[64,1024]{1,0:T(8,128)S(1)}, f32[64,1024]{1,0:T(8,128)S(1)}, u32[]{:S(2)}, u32[]{:S(2)}) collective-permute-start(f32[64,1024]{1,0:T(8,128)S(1)} %fusion.8), channel_id=1, source_target_pairs={{1,0},{2,1},{3,2},{4,3},{5,4},{6,5},{7,6},{8,7},{9,8},{10,9},{11,1... | collective-permute-start | bytes 786440 | tf_op jit(solution)/shard_map/ppermute | solution.py:15
  23.5 9.5 %collective-permute-start.3 = (f32[64,1024]{1,0:T(8,128)S(1)}, f32[64,1024]{1,0:T(8,128)S(1)}, u32[]{:S(2)}, u32[]{:S(2)}) collective-permute-start(f32[64,1024]{1,0:T(8,128)S(1)} %fusion.13), channel_id=1, source_target_pairs={{0,1},{1,2},{2,3},{3,4},{4,5},{5,6},{6,7},{7,8},{8,9},{9,10},{10,1... | collective-permute-start | bytes 786440 | tf_op jit(solution)/shard_map/ppermute | solution.py:15
  68.6 9.8 %copy-start.1 = (f32[1024,1024]{1,0:T(8,128)S(1)}, f32[1024,1024]{1,0:T(8,128)}, u32[]{:S(2)}) copy-start(f32[1024,1024]{1,0:T(8,128)} %param.6) | copy-start | bytes 12582916
  68.7 13.9 %copy-start.4 = (f32[1024,1024]{1,0:T(8,128)S(1)}, f32[1024,1024]{1,0:T(8,128)}, u32[]{:S(2)}) copy-start(f32[1024,1024]{1,0:T(8,128)} %param.5) | copy-start | bytes 12582916
  68.7 9.7 %collective-permute-start.4 = (f32[64,1024]{1,0:T(8,128)S(1)}, f32[64,1024]{1,0:T(8,128)S(1)}, u32[]{:S(2)}, u32[]{:S(2)}) collective-permute-start(f32[64,1024]{1,0:T(8,128)S(1)} %multiply_subtract_fusion.2), channel_id=1, source_target_pairs={{1,0},{2,1},{3,2},{4,3},{5,4},{6,5},{7,6},{8,7},{9,8},{10,9},{11,1... | collective-permute-start | bytes 786440 | tf_op jit(solution)/shard_map/ppermute | solution.py:15
  75.9 6.7 %collective-permute-start.5 = (f32[64,1024]{1,0:T(8,128)S(1)}, f32[64,1024]{1,0:T(8,128)S(1)}, u32[]{:S(2)}, u32[]{:S(2)}) collective-permute-start(f32[64,1024]{1,0:T(8,128)S(1)} %fusion.15), channel_id=1, source_target_pairs={{0,1},{1,2},{2,3},{3,4},{4,5},{5,6},{6,7},{7,8},{8,9},{9,10},{10,1... | collective-permute-start | bytes 786440 | tf_op jit(solution)/shard_map/ppermute | solution.py:15
  114.9 9.7 %copy-start.5 = (f32[1024,1024]{1,0:T(8,128)S(1)}, f32[1024,1024]{1,0:T(8,128)}, u32[]{:S(2)}) copy-start(f32[1024,1024]{1,0:T(8,128)} %param.5) | copy-start | bytes 12582916
  115.0 12.3 %copy-start.2 = (f32[1024,1024]{1,0:T(8,128)S(1)}, f32[1024,1024]{1,0:T(8,128)}, u32[]{:S(2)}) copy-start(f32[1024,1024]{1,0:T(8,128)} %param.6) | copy-start | bytes 12582916
  120.0 7.3 %collective-permute-start.6 = (f32[64,1024]{1,0:T(8,128)S(1)}, f32[64,1024]{1,0:T(8,128)S(1)}, u32[]{:S(2)}, u32[]{:S(2)}) collective-permute-start(f32[64,1024]{1,0:T(8,128)S(1)} %multiply_subtract_fusion.1), channel_id=1, source_target_pairs={{1,0},{2,1},{3,2},{4,3},{5,4},{6,5},{7,6},{8,7},{9,8},{10,9},{11,1... | collective-permute-start | bytes 786440 | tf_op jit(solution)/shard_map/ppermute | solution.py:15
  121.3 6.0 %collective-permute-start.7 = (f32[64,1024]{1,0:T(8,128)S(1)}, f32[64,1024]{1,0:T(8,128)S(1)}, u32[]{:S(2)}, u32[]{:S(2)}) collective-permute-start(f32[64,1024]{1,0:T(8,128)S(1)} %fusion.17), channel_id=1, source_target_pairs={{0,1},{1,2},{2,3},{3,4},{4,5},{5,6},{6,7},{7,8},{8,9},{9,10},{10,1... | collective-permute-start | bytes 786440 | tf_op jit(solution)/shard_map/ppermute | solution.py:15
where the time goes:
time: 164 us
  blocking collectives  93.2 us (57%)
  matrix products  47.9 us (29%)
  starting transfers between devices  20.2 us (12%)
    psum x3, blocking collectives, paired(): lax.psum((jnp.sum(residual * residual, axis=1, keepdims=True), jnp.sum(re...  93.2 us
    dot_general x8, matrix products, product(): jnp.dot(left, right, precision=HIGH, preferred_element_type=jnp.float32)  31.2 us
    ppermute x8, starting transfers between devices, shifted(): return lax.ppermute(block, axis, route)  20.2 us
    dot_general x4, matrix products, product_across(): lax.dot_general(left, right, (((1,), (1,)), ((), ())), precision=HIGH, pr...  16.8 us
  transfers between devices with their start and end apart: 8, of which 0 were waited for; matrix products, arithmetic and copies ran while one was open for 18% of the time, Pallas kernels for 0%

commit v1 on v0

v1 whole, which is shorter than its diff:
```python
import functools
import jax
import jax.numpy as jnp
from jax import lax
from jax.experimental import pallas as pl
from jax.experimental.pallas import tpu as pltpu
from jax.sharding import PartitionSpec as P

ITERS = 3
GROUPS = 2
TILE = 256
F32 = jnp.float32
BF16 = jnp.bfloat16
ROWS = (((1,), (0,)), ((), ()))
ACROSS = (((1,), (1,)), ((), ()))


def halves(value):
    high = value.astype(BF16)
    return high, (value - high.astype(F32)).astype(BF16)


def scalars(moment, ridge):
    def weigh(left, right, at):
        total = 0.0
        for i, a in enumerate(left):
            for j, b in enumerate(right):
                total = total + a * b * at(i + j)
        return total

    image_moment = lambda i: ridge * moment[i] + moment[i + 1]
    residual = [jnp.ones_like(ridge)]
    direction = residual
    update = [jnp.zeros_like(ridge)] * ITERS
    norm_now = moment[0]
    for step in range(ITERS):
        alpha = norm_now / weigh(direction, direction, image_moment)
        for i, e in enumerate(direction):
            update[i] = update[i] + alpha * e
        along = [ridge * e for e in direction] + [0.0]
        for i, e in enumerate(direction):
            along[i + 1] = along[i + 1] + e
        residual = residual + [0.0]
        residual = [c - alpha * a for c, a in zip(residual, along)]
        if step + 1 < ITERS:
            norm_next = weigh(residual, residual, lambda i: moment[i])
            ratio = norm_next / norm_now
            direction = [c + ratio * e for c, e in zip(residual, direction + [0.0])]
            norm_now = norm_next
    return update, residual


def kernel(
    n, slots, local_hbm, next_hbm, shrink_ref, marginal_ref, warm_ref, x_ref, r_ref,
    stage, lhi, llo, nhi, nlo, basis, total, vcat, upcat, upper, psend, precv,
    square, mine, others,
    load_sem, vs_sem, vr_sem, ps_sem, pr_sem, ms_sem, mr_sem,
):
    me = lax.axis_index("snp")
    traits, block = warm_ref.shape
    count = traits // GROUPS
    tiles = block // TILE
    barrier = pltpu.get_barrier_semaphore()
    for k in range(1, n):
        pl.semaphore_signal(barrier, inc=1, device_id={"snp": lax.rem(me + k, n)})

    def load(i):
        source, width = (next_hbm, (i + 1) * TILE) if i < tiles else (local_hbm, block)
        rows = pl.ds((i % tiles) * TILE, TILE)
        cols = pl.ds(0, width)
        slot = i % slots
        return pltpu.make_async_copy(
            source.at[rows, cols], stage.at[slot, :, cols], load_sem.at[slot]
        )

    for i in range(slots):
        load(i).start()

    def convert(i):
        load(i).wait()
        row = (i % tiles) * TILE
        width = (i + 1) * TILE if i < tiles else block
        for c in range(0, width, TILE):
            piece = stage[i % slots, :, c : c + TILE]
            if i >= tiles and c == row:
                a = lax.broadcasted_iota(jnp.int32, (TILE, TILE), 0)
                b = lax.broadcasted_iota(jnp.int32, (TILE, TILE), 1)
                piece = jnp.where(a == b, 0.0, piece)
            high, low = halves(piece)
            to_high, to_low = (nhi, nlo) if i < tiles else (lhi, llo)
            to_high[row : row + TILE, c : c + TILE] = high
            to_low[row : row + TILE, c : c + TILE] = low
        if i + slots < 2 * tiles:
            load(i + slots).start()

    def group(g):
        return pl.ds(g * count, count)

    def send_field(j, g):
        source = warm_ref.at[group(g)] if j == 0 else basis.at[j - 1, group(g)]
        return pltpu.make_async_remote_copy(
            src_ref=source, dst_ref=upper.at[j, group(g)],
            send_sem=vs_sem.at[j, g], recv_sem=vr_sem.at[j, g],
            device_id={"snp": jnp.maximum(me - 1, 0)},
        )

    def send_coupling(j, g):
        return pltpu.make_async_remote_copy(
            src_ref=psend.at[j, group(g)], dst_ref=precv.at[j, group(g)],
            send_sem=ps_sem.at[j, g], recv_sem=pr_sem.at[j, g],
            device_id={"snp": jnp.minimum(me + 1, n - 1)},
        )

    def times(left, g, high, low, dims, lo_k, hi_k):
        both = lax.dot_general(left[g, :, lo_k:hi_k], high, dims, preferred_element_type=F32)
        rest = lax.dot_general(left[g, :count, lo_k:hi_k], low, dims, preferred_element_type=F32)
        return both[:count] + both[count:] + rest

    def split_into(dest, g, value):
        high, low = halves(value)
        dest[g, :count] = high
        dest[g, count:] = low

    def field(j, g):
        return warm_ref[g * count : (g + 1) * count] if j == 0 else basis[j - 1, g * count : (g + 1) * count]

    def start_field(j, g):
        @pl.when(me > 0)
        def _():
            send_field(j, g).start()

    def coupling(j, g):
        split_into(vcat, g, field(j, g))
        for c in range(0, block, TILE):
            psend[j, g * count : (g + 1) * count, c : c + TILE] = times(
                vcat, g, nhi[c:, c : c + TILE], nlo[c:, c : c + TILE], ROWS, c, block
            )

        @pl.when(me < n - 1)
        def _():
            send_coupling(j, g).start()

    def own(j, g):
        for c in range(0, block, TILE):
            total[g, :, c : c + TILE] = times(
                vcat, g, lhi[:, c : c + TILE], llo[:, c : c + TILE], ROWS, 0, block
            )

    def finish(j, g):
        rows = slice(g * count, (g + 1) * count)

        @pl.when(me < n - 1)
        def _():
            send_field(j, g).wait_recv()

        split_into(upcat, g, upper[j, rows])
        for c in range(0, block, TILE):
            end = c + TILE
            total[g, :, c:end] += times(upcat, g, nhi[c:end, :end], nlo[c:end, :end], ACROSS, 0, end)

        @pl.when(me > 0)
        def _():
            send_coupling(j, g).wait_recv()

        image = total[g] + precv[j, rows]
        if j == 0:
            image = marginal_ref[rows] - (1.0 + shrink_ref[rows]) * warm_ref[rows] - image
        basis[j, rows] = image

    @pl.when(me == 0)
    def _():
        precv[...] = jnp.zeros_like(precv)

    @pl.when(me == n - 1)
    def _():
        upper[...] = jnp.zeros_like(upper)

    pl.semaphore_wait(barrier, n - 1)
    for g in range(GROUPS):
        start_field(0, g)
    for i in range(tiles):
        convert(i)
    for g in range(GROUPS):
        coupling(0, g)
    for i in range(tiles, 2 * tiles):
        convert(i)
    for g in range(GROUPS):
        own(0, g)
    for j in range(ITERS + 1):
        for g in range(GROUPS):
            finish(j, g)
            if j < ITERS:
                start_field(j + 1, g)
                coupling(j + 1, g)
                own(j + 1, g)

    lane = lax.broadcasted_iota(jnp.int32, (traits, 128), 1)
    table = jnp.where(lane == 6, 1.0 + shrink_ref[...], 0.0)
    for k in range(2 * ITERS):
        sums = jnp.sum(basis[k // 2] * basis[(k + 1) // 2], axis=1, keepdims=True)
        table = jnp.where(lane == k, sums, table)
    square[...] = jnp.zeros_like(square)
    square[:traits] = table
    flat = jnp.transpose(square[...])
    mine[...] = flat[:8]
    others[me] = flat[:8]

    def send_sums(k):
        return pltpu.make_async_remote_copy(
            src_ref=mine, dst_ref=others.at[me],
            send_sem=ms_sem.at[k], recv_sem=mr_sem.at[me],
            device_id={"snp": lax.rem(me + k, n)},
        )

    def take_sums(k):
        source = lax.rem(me + k, n)
        return pltpu.make_async_remote_copy(
            src_ref=mine, dst_ref=others.at[source],
            send_sem=ms_sem.at[k], recv_sem=mr_sem.at[source],
            device_id={"snp": source},
        )

    for k in range(1, n):
        send_sums(k).start()
    for k in range(1, n):
        take_sums(k).wait_recv()
    sums = others[0]
    for k in range(1, n):
        sums = sums + others[k]
    moment = [sums[k : k + 1] for k in range(2 * ITERS)]
    update, residual = scalars(moment, mine[6:7])
    for k, row in enumerate(update + residual):
        square[k : k + 1] = row
    tall = jnp.transpose(square[...])[:traits]
    x = warm_ref[...]
    for k in range(ITERS):
        x = x + tall[:, k : k + 1] * basis[k]
    x_ref[...] = x
    r = tall[:, ITERS : ITERS + 1] * basis[0]
    for k in range(1, ITERS + 1):
        r = r + tall[:, ITERS + k : ITERS + k + 1] * basis[k]
    r_ref[...] = r

    for k in range(1, n):
        send_sums(k).wait_send()

    @pl.when(me > 0)
    def _():
        for j in range(ITERS + 1):
            for g in range(GROUPS):
                send_field(j, g).wait_send()

    @pl.when(me < n - 1)
    def _():
        for j in range(ITERS + 1):
            for g in range(GROUPS):
                send_coupling(j, g).wait_send()


def on_device(local_block, next_block, shrinkage, marginal, warm_start):
    n = lax.axis_size("snp")
    traits, block = warm_start.shape
    count = traits // GROUPS
    slots = min(2 * (block // TILE), 8 if block <= 1024 else 4)
    apps = ITERS + 1
    vmem = pl.BlockSpec(memory_space=pltpu.VMEM)
    field = (apps, traits, block)
    return pl.pallas_call(
        functools.partial(kernel, n, slots),
        name="cg",
        out_shape=[jax.ShapeDtypeStruct((traits, block), F32)] * 2,
        in_specs=[pl.BlockSpec(memory_space=pltpu.HBM)] * 2 + [vmem] * 3,
        out_specs=[vmem] * 2,
        scratch_shapes=[
            pltpu.VMEM((slots, TILE, block), F32),
            pltpu.VMEM((block, block), BF16),
            pltpu.VMEM((block, block), BF16),
            pltpu.VMEM((block, block), BF16),
            pltpu.VMEM((block, block), BF16),
            pltpu.VMEM(field, F32),
            pltpu.VMEM((GROUPS, count, block), F32),
            pltpu.VMEM((GROUPS, 2 * count, block), BF16),
            pltpu.VMEM((GROUPS, 2 * count, block), BF16),
            pltpu.VMEM(field, F32),
            pltpu.VMEM(field, F32),
            pltpu.VMEM(field, F32),
            pltpu.VMEM((128, 128), F32),
            pltpu.VMEM((8, 128), F32),
            pltpu.VMEM((n, 8, 128), F32),
            pltpu.SemaphoreType.DMA((slots,)),
            pltpu.SemaphoreType.DMA((apps, GROUPS)),
            pltpu.SemaphoreType.DMA((apps, GROUPS)),
            pltpu.SemaphoreType.DMA((apps, GROUPS)),
            pltpu.SemaphoreType.DMA((apps, GROUPS)),
            pltpu.SemaphoreType.DMA((n,)),
            pltpu.SemaphoreType.DMA((n,)),
        ],
        compiler_params=pltpu.CompilerParams(
            collective_id=0, has_side_effects=True, vmem_limit_bytes=67043328
        ),
    )(local_block, next_block, shrinkage, marginal, warm_start)


def solution(mesh):
    return jax.shard_map(
        on_device,
        mesh=mesh,
        in_specs=(
            P(("parts", "snp"), None),
            P(("parts", "snp"), None),
            P(),
            P(None, ("parts", "snp")),
            P(None, ("parts", "snp")),
        ),
        out_specs=(P(None, ("parts", "snp")), P(None, ("parts", "snp"))),
        check_vma=False,
    )
```

time: 164 us -> 44.5 us (0.27)
  blocking collectives: 93.2 us -> 0 us
  matrix products: 47.9 us -> 0 us
  Pallas kernels: 0 us -> 39 us
  starting transfers between devices: 20.2 us -> 0 us
  local copies, waits for them, and re-layouts: 0.05 us -> 4.7 us
    psum x3 -> x0, blocking collectives: 93.2 us -> none  [paired(): lax.psum((jnp.sum(residual * residual, axis=1, keepdims=True), jnp.sum(re...]
    dot_general x12 -> x0, matrix products: 47.9 us -> none  [the longest x8 31.2 us: product(): jnp.dot(left, right, precision=HIGH, preferred_element_type=jnp.float32)]
    pallas_call x0 -> x1, Pallas kernels: none -> 39 us  [on_device(): pl.pallas_call(functools.partial(kernel, n, slots), name='cg', out_shape=...]
    ppermute x8 -> x0, starting transfers between devices: 20.2 us -> none  [shifted(): return lax.ppermute(block, axis, route)]
    unnamed x18 -> x3, local copies, waits for them, and re-layouts: 0.05 us -> 4.7 us
  transfers between devices with their start and end apart: 8 -> 0, of which waited for: 0 -> 0; matrix products, arithmetic and copies ran while one was open for 18% -> 0% of each run, Pallas kernels for 0% -> 0%
where the time goes in v1:
time: 44.5 us; the launch traced here: 44.3 us
  Pallas kernels  39 us (88%)
  local copies, waits for them, and re-layouts  4.7 us (11%)
  between operations  0.64 us (1%)
    pallas_call x1, Pallas kernels, on_device(): pl.pallas_call(functools.partial(kernel, n, slots), name='cg', out_shape=...  39 us
    unnamed x3, local copies, waits for them, and re-layouts  4.7 us

profile of v1, /device:TPU:0, one launch (start us, length us, event | category | flops | bytes accessed | tf_op | source)
XLA Modules:
  0.0 44.3 jit_solution(2360843180255344392)
XLA Ops:
  0.6 1.4 %copy.7.shrink_ref = f32[64,1]{1,0:T(8,128)} copy(f32[64,1]{0,1:T(1,128)} %param.7) | data formatting | bytes 512 | tf_op args[2]
  2.0 39.0 %cg.1 = (f32[64,1024]{1,0:T(8,128)}, f32[64,1024]{1,0:T(8,128)}) custom-call(f32[1024,1024]{1,0:T(8,128)} %local_hbm.1, f32[1024,1024]{1,0:T(8,128)} %next_hbm.1, f32[64,1]{1,0:T(8,128)} %copy.7.shrink_ref, f32[64,1024]{1,0:T(8,128)} %marginal_ref.1, f32[64,1024]{1,0:T(8,128)} %warm_ref.1), custom_call_target="tpu_custom_call" | custom-call | tf_op jit(solution)/shard_map/cg/pallas_call | solution.py:268
  41.0 1.7 %copy.10 = f32[64,1024]{1,0:T(8,128)} copy(f32[64,1024]{1,0:T(8,128)} %get-tuple-element.4) | data formatting | bytes 524288
  42.6 1.7 %copy.11 = f32[64,1024]{1,0:T(8,128)} copy(f32[64,1024]{1,0:T(8,128)} %get-tuple-element.5) | data formatting | bytes 524288

commit v2 on v1

--- a/solution.py
+++ b/solution.py
@@ -53,7 +53,7 @@
 def kernel(
     n, slots, local_hbm, next_hbm, shrink_ref, marginal_ref, warm_ref, x_ref, r_ref,
     stage, lhi, llo, nhi, nlo, basis, total, vcat, upcat, upper, psend, precv,
-    square, mine, others,
+    square, table, ridge, mine, others,
     load_sem, vs_sem, vr_sem, ps_sem, pr_sem, ms_sem, mr_sem,
 ):
     me = lax.axis_index("snp")
@@ -63,6 +63,11 @@
     barrier = pltpu.get_barrier_semaphore()
     for k in range(1, n):
         pl.semaphore_signal(barrier, inc=1, device_id={"snp": lax.rem(me + k, n)})
+
+    lane = lax.broadcasted_iota(jnp.int32, (count, 128), 1)
+    square[...] = jnp.zeros_like(square)
+    square[0:1, :traits] = 1.0 + shrink_ref[...]
+    ridge[...] = jnp.transpose(square[...])[:traits]
 
     def load(i):
         source, width = (next_hbm, (i + 1) * TILE) if i < tiles else (local_hbm, block)
@@ -146,7 +151,7 @@
                 vcat, g, lhi[:, c : c + TILE], llo[:, c : c + TILE], ROWS, 0, block
             )
 
-    def finish(j, g):
+    def meet(j, g):
         rows = slice(g * count, (g + 1) * count)
 
         @pl.when(me < n - 1)
@@ -154,9 +159,20 @@
             send_field(j, g).wait_recv()
 
         split_into(upcat, g, upper[j, rows])
+        last = jnp.zeros((count, TILE), F32)
         for c in range(0, block, TILE):
             end = c + TILE
-            total[g, :, c:end] += times(upcat, g, nhi[c:end, :end], nlo[c:end, :end], ACROSS, 0, end)
+            forward = times(upcat, g, nhi[c:end, :end], nlo[c:end, :end], ACROSS, 0, end)
+            image = total[g, :, c:end] + forward
+            if j == ITERS:
+                last += basis[j - 1, rows, c:end] * (image + forward)
+            total[g, :, c:end] = image
+        if j == ITERS:
+            last = jnp.sum(last, axis=1, keepdims=True)
+            table[rows] = jnp.where(lane == 2 * ITERS - 1, last, table[rows])
+
+    def finish(j, g):
+        rows = slice(g * count, (g + 1) * count)
 
         @pl.when(me > 0)
         def _():
@@ -164,8 +180,16 @@
 
         image = total[g] + precv[j, rows]
         if j == 0:
-            image = marginal_ref[rows] - (1.0 + shrink_ref[rows]) * warm_ref[rows] - image
+            image = marginal_ref[rows] - ridge[rows, :1] * warm_ref[rows] - image
         basis[j, rows] = image
+
+    def moments(g):
+        rows = slice(g * count, (g + 1) * count)
+        kept = jnp.where(lane == 2 * ITERS, ridge[rows, :1], 0.0)
+        for k in range(2 * ITERS - 1):
+            sums = jnp.sum(basis[k // 2, rows] * basis[(k + 1) // 2, rows], axis=1, keepdims=True)
+            kept = jnp.where(lane == k, sums, kept)
+        table[rows] = kept
 
     @pl.when(me == 0)
     def _():
@@ -186,21 +210,19 @@
         convert(i)
     for g in range(GROUPS):
         own(0, g)
-    for j in range(ITERS + 1):
+    for j in range(ITERS):
         for g in range(GROUPS):
+            meet(j, g)
             finish(j, g)
-            if j < ITERS:
-                start_field(j + 1, g)
-                coupling(j + 1, g)
-                own(j + 1, g)
-
-    lane = lax.broadcasted_iota(jnp.int32, (traits, 128), 1)
-    table = jnp.where(lane == 6, 1.0 + shrink_ref[...], 0.0)
-    for k in range(2 * ITERS):
-        sums = jnp.sum(basis[k // 2] * basis[(k + 1) // 2], axis=1, keepdims=True)
-        table = jnp.where(lane == k, sums, table)
-    square[...] = jnp.zeros_like(square)
-    square[:traits] = table
+            start_field(j + 1, g)
+            coupling(j + 1, g)
+            own(j + 1, g)
+            if j + 1 == ITERS:
+                moments(g)
+    for g in range(GROUPS):
+        meet(ITERS, g)
+
+    square[:traits] = table[...]
     flat = jnp.transpose(square[...])
     mine[...] = flat[:8]
     others[me] = flat[:8]
@@ -222,13 +244,15 @@
 
     for k in range(1, n):
         send_sums(k).start()
+    for g in range(GROUPS):
+        finish(ITERS, g)
     for k in range(1, n):
         take_sums(k).wait_recv()
     sums = others[0]
     for k in range(1, n):
         sums = sums + others[k]
     moment = [sums[k : k + 1] for k in range(2 * ITERS)]
-    update, residual = scalars(moment, mine[6:7])
+    update, residual = scalars(moment, mine[2 * ITERS : 2 * ITERS + 1])
     for k, row in enumerate(update + residual):
         square[k : k + 1] = row
     tall = jnp.transpose(square[...])[:traits]
@@ -285,6 +309,8 @@
             pltpu.VMEM(field, F32),
             pltpu.VMEM(field, F32),
             pltpu.VMEM((128, 128), F32),
+            pltpu.VMEM((traits, 128), F32),
+            pltpu.VMEM((traits, 128), F32),
             pltpu.VMEM((8, 128), F32),
             pltpu.VMEM((n, 8, 128), F32),
             pltpu.SemaphoreType.DMA((slots,)),
@@ -296,9 +322,9 @@
             pltpu.SemaphoreType.DMA((n,)),
         ],
         compiler_params=pltpu.CompilerParams(
-            collective_id=0, has_side_effects=True, vmem_limit_bytes=67043328
+            collective_id=0, has_side_effects=True, vmem_limit_bytes=61 << 20
         ),
-    )(local_block, next_block, shrinkage, marginal, warm_start)
+    )(local_block, next_block, shrinkage.reshape(1, traits), marginal, warm_start)
 
 
 def solution(mesh):

time: 44.5 us -> 42.8 us (0.962)
  local copies, waits for them, and re-layouts: 4.7 us -> 3.34 us
    unnamed x3 -> x2, local copies, waits for them, and re-layouts: 4.7 us -> 3.34 us
where the time goes in v2:
time: 42.8 us; the launch traced here: 42.6 us
  Pallas kernels  38.6 us (90%)
  local copies, waits for them, and re-layouts  3.34 us (8%)
  between operations  0.64 us (1%)
    pallas_call x1, Pallas kernels, on_device(): pl.pallas_call(functools.partial(kernel, n, slots), name='cg', out_shape=...  38.6 us
    unnamed x2, local copies, waits for them, and re-layouts  3.34 us

profile of v2, /device:TPU:0, one launch (start us, length us, event | category | flops | bytes accessed | tf_op | source)
XLA Modules:
  0.0 42.6 jit_solution(2583507296441769108)
XLA Ops:
  0.6 38.6 %cg.1 = (f32[64,1024]{1,0:T(8,128)}, f32[64,1024]{1,0:T(8,128)}) custom-call(f32[1024,1024]{1,0:T(8,128)} %local_hbm.1, f32[1024,1024]{1,0:T(8,128)} %next_hbm.1, f32[1,64]{1,0:T(1,128)} %bitcast.1, f32[64,1024]{1,0:T(8,128)} %marginal_ref.1, f32[64,1024]{1,0:T(8,128)} %warm_ref.1), custom_call_target="tpu_custom_call" | custom-call | tf_op jit(solution)/shard_map/cg/pallas_call | solution.py:292
  39.3 1.7 %copy.9 = f32[64,1024]{1,0:T(8,128)} copy(f32[64,1024]{1,0:T(8,128)} %get-tuple-element.4) | data formatting | bytes 524288
  40.9 1.7 %copy.10 = f32[64,1024]{1,0:T(8,128)} copy(f32[64,1024]{1,0:T(8,128)} %get-tuple-element.5) | data formatting | bytes 524288

commit v3 on v2

--- a/solution.py
+++ b/solution.py
@@ -51,15 +51,17 @@
 
 
 def kernel(
-    n, slots, local_hbm, next_hbm, shrink_ref, marginal_ref, warm_ref, x_ref, r_ref,
-    stage, lhi, llo, nhi, nlo, basis, total, vcat, upcat, upper, psend, precv,
+    n, slots, local_hbm, next_hbm, shrink_ref, marginal_hbm, warm_hbm, x_ref, r_ref,
+    marginal_ref, warm_ref, stage, lhi, llo, nhi, nlo, basis, total, vcat, upcat, upper, psend, precv,
     square, table, ridge, mine, others,
-    load_sem, vs_sem, vr_sem, ps_sem, pr_sem, ms_sem, mr_sem,
+    field_sem, load_sem, vs_sem, vr_sem, ps_sem, pr_sem, ms_sem, mr_sem,
 ):
     me = lax.axis_index("snp")
     traits, block = warm_ref.shape
     count = traits // GROUPS
     tiles = block // TILE
+    warm_load = pltpu.make_async_copy(warm_hbm, warm_ref, field_sem.at[0])
+    warm_load.start()
     barrier = pltpu.get_barrier_semaphore()
     for k in range(1, n):
         pl.semaphore_signal(barrier, inc=1, device_id={"snp": lax.rem(me + k, n)})
@@ -80,6 +82,8 @@
 
     for i in range(slots):
         load(i).start()
+    marginal_load = pltpu.make_async_copy(marginal_hbm, marginal_ref, field_sem.at[1])
+    marginal_load.start()
 
     def convert(i):
         load(i).wait()
@@ -199,17 +203,19 @@
     def _():
         upper[...] = jnp.zeros_like(upper)
 
-    pl.semaphore_wait(barrier, n - 1)
-    for g in range(GROUPS):
-        start_field(0, g)
+    warm_load.wait()
     for i in range(tiles):
         convert(i)
+    pl.semaphore_wait(barrier, n - 1)
+    for g in range(GROUPS):
+        start_field(0, g)
     for g in range(GROUPS):
         coupling(0, g)
     for i in range(tiles, 2 * tiles):
         convert(i)
     for g in range(GROUPS):
         own(0, g)
+    marginal_load.wait()
     for j in range(ITERS):
         for g in range(GROUPS):
             meet(j, g)
@@ -244,8 +250,6 @@
 
     for k in range(1, n):
         send_sums(k).start()
-    for g in range(GROUPS):
-        finish(ITERS, g)
     for k in range(1, n):
         take_sums(k).wait_recv()
     sums = others[0]
@@ -260,10 +264,20 @@
     for k in range(ITERS):
         x = x + tall[:, k : k + 1] * basis[k]
     x_ref[...] = x
-    r = tall[:, ITERS : ITERS + 1] * basis[0]
-    for k in range(1, ITERS + 1):
-        r = r + tall[:, ITERS + k : ITERS + k + 1] * basis[k]
-    r_ref[...] = r
+    for g in range(GROUPS):
+        rows = slice(g * count, (g + 1) * count)
+        r = tall[rows, 2 * ITERS : 2 * ITERS + 1] * total[g]
+        for k in range(ITERS):
+            r = r + tall[rows, ITERS + k : ITERS + k + 1] * basis[k, rows]
+        r_ref[rows] = r
+    for g in range(GROUPS):
+        rows = slice(g * count, (g + 1) * count)
+
+        @pl.when(me > 0)
+        def _():
+            send_coupling(ITERS, g).wait_recv()
+
+        r_ref[rows] += tall[rows, 2 * ITERS : 2 * ITERS + 1] * precv[ITERS, rows]
 
     for k in range(1, n):
         send_sums(k).wait_send()
@@ -279,6 +293,11 @@
         for j in range(ITERS + 1):
             for g in range(GROUPS):
                 send_coupling(j, g).wait_send()
+
+
+def hand_on(x_in, r_in, x_ref, r_ref):
+    x_ref[...] = x_in[...]
+    r_ref[...] = r_in[...]
 
 
 def on_device(local_block, next_block, shrinkage, marginal, warm_start):
@@ -288,20 +307,23 @@
     slots = min(2 * (block // TILE), 8 if block <= 1024 else 4)
     apps = ITERS + 1
     vmem = pl.BlockSpec(memory_space=pltpu.VMEM)
+    hbm = pl.BlockSpec(memory_space=pltpu.HBM)
     field = (apps, traits, block)
-    return pl.pallas_call(
+    x, r = pl.pallas_call(
         functools.partial(kernel, n, slots),
         name="cg",
         out_shape=[jax.ShapeDtypeStruct((traits, block), F32)] * 2,
-        in_specs=[pl.BlockSpec(memory_space=pltpu.HBM)] * 2 + [vmem] * 3,
+        in_specs=[hbm, hbm, vmem, hbm, hbm],
         out_specs=[vmem] * 2,
         scratch_shapes=[
+            pltpu.VMEM((traits, block), F32),
+            pltpu.VMEM((traits, block), F32),
             pltpu.VMEM((slots, TILE, block), F32),
             pltpu.VMEM((block, block), BF16),
             pltpu.VMEM((block, block), BF16),
             pltpu.VMEM((block, block), BF16),
             pltpu.VMEM((block, block), BF16),
-            pltpu.VMEM(field, F32),
+            pltpu.VMEM((ITERS, traits, block), F32),
             pltpu.VMEM((GROUPS, count, block), F32),
             pltpu.VMEM((GROUPS, 2 * count, block), BF16),
             pltpu.VMEM((GROUPS, 2 * count, block), BF16),
@@ -313,6 +335,7 @@
             pltpu.VMEM((traits, 128), F32),
             pltpu.VMEM((8, 128), F32),
             pltpu.VMEM((n, 8, 128), F32),
+            pltpu.SemaphoreType.DMA((2,)),
             pltpu.SemaphoreType.DMA((slots,)),
             pltpu.SemaphoreType.DMA((apps, GROUPS)),
             pltpu.SemaphoreType.DMA((apps, GROUPS)),
@@ -325,6 +348,13 @@
             collective_id=0, has_side_effects=True, vmem_limit_bytes=61 << 20
         ),
     )(local_block, next_block, shrinkage.reshape(1, traits), marginal, warm_start)
+    return pl.pallas_call(
+        hand_on,
+        name="hand_on",
+        out_shape=[jax.ShapeDtypeStruct((traits, block), F32)] * 2,
+        in_specs=[vmem] * 2,
+        out_specs=[vmem] * 2,
+    )(x, r)
 
 
 def solution(mesh):

time: 42.8 us -> 40.8 us (0.953)
  local copies, waits for them, and re-layouts: 3.34 us -> 0 us
  Pallas kernels: 38.6 us -> 40 us
    unnamed x2 -> x0, local copies, waits for them, and re-layouts: 3.34 us -> none
    pallas_call x0 -> x1, Pallas kernels: none -> 1.84 us  [on_device(): pl.pallas_call(hand_on, name='hand_on', out_shape=[jax.ShapeDtypeStruct((...]
    pallas_call x1, Pallas kernels: 38.6 us -> 38.1 us  [on_device(): pl.pallas_call(functools.partial(kernel, n, slots), name='cg', out_shape=...]
where the time goes in v3:
time: 40.8 us; the launch traced here: 40.6 us
  Pallas kernels  40 us (98%)
  between operations  0.64 us (2%)
    pallas_call x1, Pallas kernels, on_device(): pl.pallas_call(functools.partial(kernel, n, slots), name='cg', out_shape=...  38.1 us
    pallas_call x1, Pallas kernels, on_device(): pl.pallas_call(hand_on, name='hand_on', out_shape=[jax.ShapeDtypeStruct((...  1.84 us

profile of v3, /device:TPU:0, one launch (start us, length us, event | category | flops | bytes accessed | tf_op | source)
XLA Modules:
  0.0 40.6 jit_solution(18305434418250636021)
XLA Ops:
  0.6 38.1 %cg.1 = (f32[64,1024]{1,0:T(8,128)}, f32[64,1024]{1,0:T(8,128)}) custom-call(f32[1024,1024]{1,0:T(8,128)} %local_hbm.1, f32[1024,1024]{1,0:T(8,128)} %next_hbm.1, f32[1,64]{1,0:T(1,128)} %bitcast.1, f32[64,1024]{1,0:T(8,128)} %marginal_hbm.1, f32[64,1024]{1,0:T(8,128)} %warm_hbm.1), custom_call_target="tpu_custom_call" | custom-call | tf_op jit(solution)/shard_map/cg/pallas_call | solution.py:312
  38.8 1.8 %hand_on.1 = (f32[64,1024]{1,0:T(8,128)}, f32[64,1024]{1,0:T(8,128)}) custom-call(f32[64,1024]{1,0:T(8,128)} %get-tuple-element.4.x_in, f32[64,1024]{1,0:T(8,128)} %get-tuple-element.5.r_in), custom_call_target="tpu_custom_call" | custom-call | tf_op jit(solution)/shard_map/hand_on/pallas_call | solution.py:351

commit v4 on v3

--- a/solution.py
+++ b/solution.py
@@ -204,11 +204,11 @@
         upper[...] = jnp.zeros_like(upper)
 
     warm_load.wait()
+    pl.semaphore_wait(barrier, n - 1)
+    for g in range(GROUPS):
+        start_field(0, g)
     for i in range(tiles):
         convert(i)
-    pl.semaphore_wait(barrier, n - 1)
-    for g in range(GROUPS):
-        start_field(0, g)
     for g in range(GROUPS):
         coupling(0, g)
     for i in range(tiles, 2 * tiles):

time: 40.8 us -> 40.9 us (level)
  no operation moved by 1% of the time
where the time goes in v4:
time: 40.9 us; the launch traced here: 40.7 us
  Pallas kernels  40.1 us (98%)
  between operations  0.64 us (2%)
    pallas_call x1, Pallas kernels, on_device(): pl.pallas_call(functools.partial(kernel, n, slots), name='cg', out_shape=...  38.3 us
    pallas_call x1, Pallas kernels, on_device(): pl.pallas_call(hand_on, name='hand_on', out_shape=[jax.ShapeDtypeStruct((...  1.84 us

profile of v4, /device:TPU:0, one launch (start us, length us, event | category | flops | bytes accessed | tf_op | source)
XLA Modules:
  0.0 40.7 jit_solution(1497911476906005687)
XLA Ops:
  0.6 38.3 %cg.1 = (f32[64,1024]{1,0:T(8,128)}, f32[64,1024]{1,0:T(8,128)}) custom-call(f32[1024,1024]{1,0:T(8,128)} %local_hbm.1, f32[1024,1024]{1,0:T(8,128)} %next_hbm.1, f32[1,64]{1,0:T(1,128)} %bitcast.1, f32[64,1024]{1,0:T(8,128)} %marginal_hbm.1, f32[64,1024]{1,0:T(8,128)} %warm_hbm.1), custom_call_target="tpu_custom_call" | custom-call | tf_op jit(solution)/shard_map/cg/pallas_call | solution.py:312
  38.9 1.8 %hand_on.1 = (f32[64,1024]{1,0:T(8,128)}, f32[64,1024]{1,0:T(8,128)}) custom-call(f32[64,1024]{1,0:T(8,128)} %get-tuple-element.4.x_in, f32[64,1024]{1,0:T(8,128)} %get-tuple-element.5.r_in), custom_call_target="tpu_custom_call" | custom-call | tf_op jit(solution)/shard_map/hand_on/pallas_call | solution.py:351
